TPU v7x, 32 devices: a whole 2x2x4 slice. The times are simulated.
32 devices in a mesh: neg: 8 (over y, x, core), qry: 4 (over z).
Axes of the slice: x: 2, y: 2, z: 4, core: 2. Of those that a mesh axis runs over, the one named last changes fastest.
Arguments:
- items_table: bfloat16 [65536, 512], P('neg'), may hold values from -6 to 6
- fetch_rows: int32 [256, 1280], P(('neg', 'qry')), may hold values from 0 to 8191, as said below
- neighbour_slots: int32 [16384, 40], P(('neg', 'qry')), may hold values from 0 to 10239, as said below
- neighbour_count: int32 [16384], P(('neg', 'qry')), may hold values from 20 to 40
- self_slot: int32 [16384], P(('neg', 'qry')), may hold values from 0 to 10239
- negative_count: int32 [16384], P('neg'), may hold values from 1 to 999
- message_weight: bfloat16 [512, 512], replicated, may hold values from -0.25 to 0.25
- message_bias: float32 [512], replicated, may hold values from -3 to 3
- self_weight: bfloat16 [512, 512], replicated, may hold values from -0.25 to 0.25
- neighbour_weight: bfloat16 [512, 512], replicated, may hold values from -0.25 to 0.25
- output_bias: float32 [512], replicated, may hold values from -3 to 3
- queries: bfloat16 [4096, 512], P('qry'), may hold values from -8 to 8
Outputs:
- negative_embed: bfloat16 [16384, 512], P(('neg', 'qry'))
- query_lse: float32 [4096], P('qry')
Inputs may be any that keep to these rules, and one draw needn't show every extreme that they name: Within one row of fetch_rows (one device's list for one partition) no item appears twice. `neighbour_slots`: every one of a device's 8 * 1280 fetched rows is named by at least one live neighbour of that device's negatives.
All inputs are finite; a program needn't handle non-finite values.
Results may differ from a plain program's by a relative error of at most 0.0055.
Values may be sent and summed in bfloat16 or wider, within the bound.
A program may use at most 128 MiB of HBM per device.

v0:
```python
import functools
import math

import jax
import jax.numpy as jnp
from jax import lax
from jax.experimental import pallas as pl
from jax.experimental.pallas import tpu as pltpu
from jax.sharding import PartitionSpec as P


LANES = 128
ROWS = 128
DEAD = 32767
NT = (((1,), (1,)), ((), ()))


def sort_pairs(count):
    full = 1
    while full < count:
        full *= 2
    pairs = []
    p = 1
    while p < full:
        k = p
        while k >= 1:
            for j in range(k % p, full - k, 2 * k):
                for i in range(min(k, full - j - k)):
                    if (i + j) // (2 * p) == (i + j + k) // (2 * p):
                        if i + j + k < count:
                            pairs.append((i + j, i + j + k))
            k //= 2
        p *= 2
    return pairs


def gather_kernel(index_ref, table_ref, *refs):
    weights, out_ref, flipped, (wide_ref, picked_ref) = refs[:3], refs[3], refs[4:7], refs[7:]
    block = pl.program_id(0)
    rows, width = table_ref.shape
    cap = out_ref.shape[1]
    pieces = width // LANES

    @pl.when(block == 0)
    def _():
        for weight, turned in zip(weights, flipped):
            turned[...] = weight[...].T

        @pl.loop(0, rows // ROWS)
        def _(t):
            span = pl.ds(pl.multiple_of(t * ROWS, ROWS), ROWS)
            for c in range(pieces):
                wide_ref[pl.ds(t * ROWS * pieces + c, ROWS, stride=pieces), :] = table_ref[
                    span, c * LANES : (c + 1) * LANES
                ].astype(jnp.float32)

    unroll = 32

    @pl.loop(0, cap // unroll)
    def _(i):
        for u in range(unroll):
            place = i * unroll + u
            row = pl.multiple_of(index_ref[block, place], pieces)
            picked_ref[pl.ds(pl.multiple_of(place * pieces, pieces), pieces), :] = wide_ref[
                pl.ds(row, pieces), :
            ]

    @pl.loop(0, cap // ROWS)
    def _(t):
        span = pl.ds(pl.multiple_of(t * ROWS, ROWS), ROWS)
        for c in range(pieces):
            out_ref[0, span, c * LANES : (c + 1) * LANES] = picked_ref[
                pl.ds(t * ROWS * pieces + c, ROWS, stride=pieces), :
            ].astype(jnp.bfloat16)


def gather_rows(index, table, weights):
    blocks, cap = index.shape
    rows, width = table.shape
    pieces = width // LANES
    return pl.pallas_call(
        gather_kernel,
        grid=(blocks,),
        out_shape=[jax.ShapeDtypeStruct((blocks, cap, width), jnp.bfloat16)]
        + [jax.ShapeDtypeStruct(w.shape[::-1], w.dtype) for w in weights],
        in_specs=[pl.BlockSpec(memory_space=pltpu.SMEM)]
        + [pl.BlockSpec(memory_space=pltpu.VMEM)] * 4,
        out_specs=[pl.BlockSpec((1, cap, width), lambda b: (b, 0, 0))]
        + [pl.BlockSpec(memory_space=pltpu.VMEM)] * 3,
        scratch_shapes=[
            pltpu.VMEM((rows * pieces, LANES), jnp.float32),
            pltpu.VMEM((cap * pieces, LANES), jnp.float32),
        ],
        compiler_params=pltpu.CompilerParams(vmem_limit_bytes=48 << 20),
    )(index * pieces, table, *weights)


def partial_kernel(
    base_ref, rows_ref, slots_ref, wm_ref, mb_ref, ws_ref, wn_ref,
    out_ref, order_ref, times_ref, counts_ref, self_hot_ref,
):
    cap = rows_ref.shape[1]
    negatives = counts_ref.shape[1]
    groups, neighbours = negatives // LANES, times_ref.shape[1]
    half = neighbours // 2
    packed = 16
    chunk = 320 if cap % 320 == 0 else ROWS
    big = jnp.int32(32767)
    base = base_ref[0]
    places = []
    live = jnp.zeros((groups, LANES), jnp.int32)
    mine = jnp.zeros((groups, LANES), jnp.int32)
    for k in range(neighbours):
        word = slots_ref[(k % half) * groups : (k % half + 1) * groups, :]
        slot = word & DEAD if k < half else word >> 16
        local = slot - base
        inside = (local >= 0) & (local < cap)
        live = live + jnp.where(slot < DEAD, 1, 0)
        mine = mine + jnp.where(inside, 1, 0)
        places.append(jnp.where(inside, local, big))
    for a, b in sort_pairs(neighbours):
        low, high = jnp.minimum(places[a], places[b]), jnp.maximum(places[a], places[b])
        places[a], places[b] = low, high
    run = jnp.ones((groups, LANES), jnp.float32)
    for k in range(neighbours):
        if k:
            run = jnp.where(places[k] == places[k - 1], run + 1.0, 1.0)
        for g in range(groups):
            tile = (packed, LANES)
            order_ref[g, k] = jnp.broadcast_to(places[k][g : g + 1], tile).astype(jnp.int16)
            times_ref[g, k] = jnp.broadcast_to(run[g : g + 1], tile).astype(jnp.bfloat16)
    inverse = 1.0 / live.astype(jnp.float32)
    own = slots_ref[half * groups : (half + 1) * groups, :] - base
    own = jnp.where((own >= 0) & (own < cap), own, big)
    iota = lax.broadcasted_iota(jnp.int32, (packed, LANES), 0)
    tiles = chunk // packed
    unroll = 4
    for g in range(groups):
        lanes = pl.ds(g * LANES, LANES)
        steps = (jnp.max(mine[g : g + 1]) + unroll - 1) // unroll
        own_tile = jnp.broadcast_to(own[g : g + 1], (packed, LANES)).astype(jnp.int16)

        @pl.loop(0, cap // chunk)
        def _(c):
            first = c * chunk
            here = [(iota + (first + packed * i)).astype(jnp.int16) for i in range(tiles)]

            def step(i, totals):
                for u in range(unroll):
                    k = unroll * i + u
                    slot, times = order_ref[g, k], times_ref[g, k]
                    totals = tuple(
                        jnp.where(here[j] == slot, times, totals[j]) for j in range(tiles)
                    )
                return totals

            zero = jnp.zeros((packed, LANES), jnp.bfloat16)
            one = jnp.ones((packed, LANES), jnp.bfloat16)
            totals = lax.fori_loop(0, steps, step, (zero,) * tiles)
            for j in range(tiles):
                span = pl.ds(pl.multiple_of(first + packed * j, packed), packed)
                counts_ref[span, lanes] = totals[j]
                self_hot_ref[span, lanes] = jnp.where(here[j] == own_tile, one, zero)

    rows = rows_ref[0]
    message = jax.nn.relu(
        lax.dot_general(wm_ref[...], rows, NT, preferred_element_type=jnp.float32) + mb_ref[...]
    ).astype(jnp.bfloat16)
    summed = jnp.dot(message, counts_ref[...], preferred_element_type=jnp.float32)
    scale = jnp.concatenate([inverse[g : g + 1, :] for g in range(groups)], axis=1)
    mean = (summed * scale).astype(jnp.bfloat16)
    own_part = lax.dot_general(ws_ref[...], rows, NT, preferred_element_type=jnp.float32).astype(
        jnp.bfloat16
    )
    part = jnp.dot(own_part, self_hot_ref[...], preferred_element_type=jnp.float32)
    part = part + jnp.dot(wn_ref[...], mean, preferred_element_type=jnp.float32)
    out_ref[...] = part.astype(jnp.bfloat16)


def partial_hidden(base, rows, which, lists, shape, wm, mb, ws, wn):
    _, cap, width = rows.shape
    negatives, neighbours = shape
    groups = negatives // LANES
    whole = pl.BlockSpec(memory_space=pltpu.VMEM)
    return pl.pallas_call(
        partial_kernel,
        grid=(1,),
        out_shape=jax.ShapeDtypeStruct((width, negatives), jnp.bfloat16),
        in_specs=[
            pl.BlockSpec(memory_space=pltpu.SMEM),
            pl.BlockSpec((1, cap, width), lambda b: (which, 0, 0)),
            whole, whole, whole, whole, whole,
        ],
        out_specs=pl.BlockSpec((width, negatives), lambda b: (0, 0)),
        scratch_shapes=[
            pltpu.VMEM((groups, neighbours, 16, LANES), jnp.int16),
            pltpu.VMEM((groups, neighbours, 16, LANES), jnp.bfloat16),
            pltpu.VMEM((cap, negatives), jnp.bfloat16),
            pltpu.VMEM((cap, negatives), jnp.bfloat16),
        ],
    )(base, rows, lists, wm, mb, ws, wn)


def score_kernel(parts, blocks, *refs):
    part_refs = refs[:parts]
    query_refs = refs[parts : parts + blocks]
    bias_ref, count_ref, embed_ref, peak_ref, total_ref = refs[parts + blocks :]
    hidden = bias_ref[...]
    for ref in part_refs:
        hidden = hidden + ref[...].astype(jnp.float32)
    hidden = jax.nn.relu(hidden)
    scale = lax.rsqrt(jnp.mean(hidden * hidden, axis=0, keepdims=True) + 0.25)
    embed_ref[...] = (hidden * scale).T.astype(jnp.bfloat16)
    log_count = jnp.log(count_ref[...].astype(jnp.float32))
    tile = 512
    for b in range(blocks):

        @pl.loop(0, query_refs[b].shape[0] // tile)
        def _(t):
            span = pl.ds(pl.multiple_of(t * tile, tile), tile)
            scores = (
                0.25
                * lax.dot_general(
                    embed_ref[...], query_refs[b][span, :], NT, preferred_element_type=jnp.float32
                )
                - log_count
            )
            peak = jnp.max(scores, axis=0, keepdims=True)
            peak_ref[b : b + 1, span] = peak
            total_ref[b : b + 1, span] = jnp.sum(jnp.exp(scores - peak), axis=0, keepdims=True)


def embed_and_score(parts, queries, bias, count):
    width, negatives = parts[0].shape
    rows = queries[0].shape[0]
    whole = pl.BlockSpec(memory_space=pltpu.VMEM)
    blocks = len(queries)
    return pl.pallas_call(
        functools.partial(score_kernel, len(parts), blocks),
        out_shape=(
            jax.ShapeDtypeStruct((negatives, width), jnp.bfloat16),
            jax.ShapeDtypeStruct((blocks, rows), jnp.float32),
            jax.ShapeDtypeStruct((blocks, rows), jnp.float32),
        ),
        in_specs=[whole] * (len(parts) + blocks + 2),
        out_specs=(whole,) * 3,
        cost_estimate=pl.CostEstimate(
            flops=2 * blocks * rows * negatives * width,
            bytes_accessed=2 * blocks * rows * width,
            transcendentals=blocks * rows * negatives,
        ),
    )(*parts, *queries, bias, count)


def swap(value, axis, offset):
    size = lax.axis_size(axis)
    if offset == 0:
        return value
    return lax.ppermute(value, axis, [(i, i ^ offset) for i in range(size)])


def per_device(
    items_table,
    fetch_rows,
    neighbour_slots,
    neighbour_count,
    self_slot,
    negative_count,
    message_weight,
    message_bias,
    self_weight,
    neighbour_weight,
    output_bias,
    queries,
):
    n_neg, n_qry = lax.axis_size("neg"), lax.axis_size("qry")
    own_neg, own_qry = lax.axis_index("neg"), lax.axis_index("qry")
    cap = fetch_rows.shape[1]
    negatives, neighbours = neighbour_slots.shape
    groups = negatives // LANES

    assert n_neg * cap < DEAD and neighbours % 4 == 0
    live = jnp.arange(neighbours, dtype=jnp.int32)[None, :] < neighbour_count[:, None]
    slots = jnp.where(live, neighbour_slots, DEAD).T
    half = neighbours // 2
    words = slots[:half] | (slots[half:] << 16)
    lists = jnp.concatenate([words.reshape(-1, LANES), self_slot.reshape(-1, LANES)])
    far = sorted(range(n_neg), key=lambda d: (-(d // 2).bit_count(), -(d % 2), -d))
    asked = {}
    for d in far:
        mine = lax.dynamic_index_in_dim(fetch_rows, own_neg ^ d, 0, keepdims=False)
        asked[d] = swap(jnp.concatenate([lists, mine.reshape(-1, LANES)]), "neg", d)
    query_blocks = [queries]
    for d in range(1, n_qry):
        query_blocks.append(swap(queries, "qry", d))

    base = (own_neg * cap).astype(jnp.int32).reshape(1)
    wanted = jnp.stack([asked[d][(half + 1) * groups :].reshape(cap) for d in far])
    rows, wm, ws, wn = gather_rows(
        wanted, items_table, (message_weight, self_weight, neighbour_weight)
    )
    parts = []
    for j, d in enumerate(far):
        part = partial_hidden(
            base, rows, j, asked[d], (negatives, neighbours), wm, message_bias[:, None], ws, wn
        )
        base, part = lax.optimization_barrier((base, part))
        parts.append(swap(part, "neg", d))

    count = lax.dynamic_slice_in_dim(negative_count, own_qry * negatives, negatives)
    negative_embed, peak, total = embed_and_score(
        parts, query_blocks, output_bias[:, None], count[:, None]
    )
    pairs = jnp.stack([peak, total], axis=1)
    pairs = jnp.stack([swap(pairs[d], "qry", d) for d in range(n_qry)])
    pairs = lax.all_gather(pairs, "neg").reshape(n_neg * n_qry, 2, -1)
    top = jnp.max(pairs[:, 0], axis=0)
    whole = jnp.sum(pairs[:, 1] * jnp.exp(pairs[:, 0] - top[None, :]), axis=0)
    query_lse = top + jnp.log(whole) - math.log(negatives * n_neg * n_qry)
    return (negative_embed, query_lse)


def solution(mesh):
    in_specs = (
        P("neg", None),
        P(("neg", "qry"), None),
        P(("neg", "qry"), None),
        P(("neg", "qry")),
        P(("neg", "qry")),
        P("neg"),
        P(),
        P(),
        P(),
        P(),
        P(),
        P("qry", None),
    )
    out_specs = (P(("neg", "qry"), None), P("qry"))
    return jax.shard_map(
        per_device, mesh=mesh, in_specs=in_specs, out_specs=out_specs, check_vma=False
    )
```

profile of v0, /device:TPU:0, one launch (start us, length us, event | category | flops | bytes accessed | tf_op | source)
XLA Modules:
  0.0 259.8 jit_solution(3898313455829984402)
XLA Ops:
  1.6 1.4 fusion.7
  3.0 1.3 pad_add_fusion.8
  4.3 3.0 %collective-permute-start.5 = (s32[94,128]{1,0:T(8,128)S(1)}, s32[94,128]{1,0:T(8,128)S(1)}, u32[]{:S(2)}, u32[]{:S(2)}) collective-permute-start(s32[94,128]{1,0:T(8,128)S(1)} %get-tuple-element.63), channel_id=1, source_target_pairs={{0,8},{4,12},{8,0},{12,4},{16,24},{20,28},{24,16},{28,20},{1,9},{5... | collective-permute-start | bytes 144392 | tf_op jit(solution)/shard_map/ppermute | solution.py:259
  7.3 1.5 collective-permute-start.4
  9.1 3.0 %collective-permute-start.1 = (s32[94,128]{1,0:T(8,128)S(1)}, s32[94,128]{1,0:T(8,128)S(1)}, u32[]{:S(2)}, u32[]{:S(2)}) collective-permute-start(s32[94,128]{1,0:T(8,128)S(1)} %get-tuple-element.59), channel_id=1, source_target_pairs={{0,24},{4,28},{8,16},{12,20},{16,8},{20,12},{24,0},{28,4},{1,25},{... | collective-permute-start | bytes 144392 | tf_op jit(solution)/shard_map/ppermute | solution.py:259
  12.7 1.5 copy.32.mb_ref
  15.6 3.2 %collective-permute-done.slots_ref = s32[94,128]{1,0:T(8,128)S(1)} collective-permute-done((s32[94,128]{1,0:T(8,128)S(1)}, s32[94,128]{1,0:T(8,128)S(1)}, u32[]{:S(2)}, u32[]{:S(2)}) %collective-permute-start) | collective-permute-done | bytes 48160 | tf_op jit(solution)/shard_map/ppermute | solution.py:259
  18.9 1.0 copy-done.3
  19.9 1.0 copy-done.4
  21.0 1.0 copy-done.5
  22.0 35.5 %shard_map.131 = (bf16[8,1280,512]{2,1,0:T(8,128)(2,1)}, bf16[512,512]{1,0:T(8,128)(2,1)S(1)}, bf16[512,512]{1,0:T(8,128)(2,1)S(1)}, bf16[512,512]{1,0:T(8,128)(2,1)S(1)}) custom-call(s32[8,1280]{1,0:T(8,128)S(1)} %broadcast_multiply_fusion.index_ref, bf16[8192,512]{1,0:T(8,128)(2,1)} %table_ref.1, bf16[512,512]{1,0:T(8,128)(2,1)S(1)} %copy-done.3, ...), custom_call_target="tpu_custom_call" | custom-call | tf_op jit(solution)/shard_map/pallas_call | solution.py:81
  59.9 8.9 %shard_map.132 = bf16[512,512]{1,0:T(8,128)(2,1)} custom-call(s32[1]{0:T(128)} %bitcast.base_ref, bf16[8,1280,512]{2,1,0:T(8,128)(2,1)} %get-tuple-element.24.rows_ref, s32[94,128]{1,0:T(8,128)} %copy-done.21, bf16[512,512]{1,0:T(8,128)(2,1)} %copy-done, f32[512,1]{1,0:T(8,128)} %copy.32.mb_ref, bf16[512,512]{1,0:T(8,128)(2,1)} %copy-done.1, ...), custom_call_target="tpu_custom_call" | custom-call | tf_op jit(solution)/shard_map/pallas_call | solution.py:185
  68.9 9.0 %shard_map.133 = bf16[512,512]{1,0:T(8,128)(2,1)} custom-call(s32[1]{0:T(128)} %bitcast.base_ref, bf16[8,1280,512]{2,1,0:T(8,128)(2,1)} %get-tuple-element.24.rows_ref, s32[94,128]{1,0:T(8,128)} %copy-done.19, bf16[512,512]{1,0:T(8,128)(2,1)} %copy-done, f32[512,1]{1,0:T(8,128)} %copy.32.mb_ref, bf16[512,512]{1,0:T(8,128)(2,1)} %copy-done.1, ...), custom_call_target="tpu_custom_call" | custom-call | tf_op jit(solution)/shard_map/pallas_call | solution.py:185
  77.9 9.0 %shard_map.134 = bf16[512,512]{1,0:T(8,128)(2,1)} custom-call(s32[1]{0:T(128)} %bitcast.base_ref, bf16[8,1280,512]{2,1,0:T(8,128)(2,1)} %get-tuple-element.24.rows_ref, s32[94,128]{1,0:T(8,128)} %copy-done.18, bf16[512,512]{1,0:T(8,128)(2,1)} %copy-done, f32[512,1]{1,0:T(8,128)} %copy.32.mb_ref, bf16[512,512]{1,0:T(8,128)(2,1)} %copy-done.1, ...), custom_call_target="tpu_custom_call" | custom-call | tf_op jit(solution)/shard_map/pallas_call | solution.py:185
  86.9 9.1 %shard_map.135 = bf16[512,512]{1,0:T(8,128)(2,1)} custom-call(s32[1]{0:T(128)} %bitcast.base_ref, bf16[8,1280,512]{2,1,0:T(8,128)(2,1)} %get-tuple-element.24.rows_ref, s32[94,128]{1,0:T(8,128)} %copy-done.17, bf16[512,512]{1,0:T(8,128)(2,1)} %copy-done, f32[512,1]{1,0:T(8,128)} %copy.32.mb_ref, bf16[512,512]{1,0:T(8,128)(2,1)} %copy-done.1, ...), custom_call_target="tpu_custom_call" | custom-call | tf_op jit(solution)/shard_map/pallas_call | solution.py:185
  96.0 8.9 %shard_map.136 = bf16[512,512]{1,0:T(8,128)(2,1)} custom-call(s32[1]{0:T(128)} %bitcast.base_ref, bf16[8,1280,512]{2,1,0:T(8,128)(2,1)} %get-tuple-element.24.rows_ref, s32[94,128]{1,0:T(8,128)} %copy-done.16, bf16[512,512]{1,0:T(8,128)(2,1)} %copy-done, f32[512,1]{1,0:T(8,128)} %copy.32.mb_ref, bf16[512,512]{1,0:T(8,128)(2,1)} %copy-done.1, ...), custom_call_target="tpu_custom_call" | custom-call | tf_op jit(solution)/shard_map/pallas_call | solution.py:185
  104.9 9.1 %shard_map.137 = bf16[512,512]{1,0:T(8,128)(2,1)} custom-call(s32[1]{0:T(128)} %bitcast.base_ref, bf16[8,1280,512]{2,1,0:T(8,128)(2,1)} %get-tuple-element.24.rows_ref, s32[94,128]{1,0:T(8,128)} %copy-done.15, bf16[512,512]{1,0:T(8,128)(2,1)} %copy-done, f32[512,1]{1,0:T(8,128)} %copy.32.mb_ref, bf16[512,512]{1,0:T(8,128)(2,1)} %copy-done.1, ...), custom_call_target="tpu_custom_call" | custom-call | tf_op jit(solution)/shard_map/pallas_call | solution.py:185
  114.0 9.1 %shard_map.138 = bf16[512,512]{1,0:T(8,128)(2,1)} custom-call(s32[1]{0:T(128)} %bitcast.base_ref, bf16[8,1280,512]{2,1,0:T(8,128)(2,1)} %get-tuple-element.24.rows_ref, s32[94,128]{1,0:T(8,128)} %copy-done.20, bf16[512,512]{1,0:T(8,128)(2,1)} %copy-done, f32[512,1]{1,0:T(8,128)} %copy.32.mb_ref, bf16[512,512]{1,0:T(8,128)(2,1)} %copy-done.1, ...), custom_call_target="tpu_custom_call" | custom-call | tf_op jit(solution)/shard_map/pallas_call | solution.py:185
  125.6 1.7 collective-permute-start.9
  127.3 2.3 collective-permute-start.14
  129.5 8.8 %collective-permute-done.12.refs_5_ = bf16[512,512]{1,0:T(8,128)(2,1)S(1)} collective-permute-done((bf16[512,512]{1,0:T(8,128)(2,1)S(1)}, bf16[512,512]{1,0:T(8,128)(2,1)S(1)}, u32[]{:S(2)}, u32[]{:S(2)}) %collective-permute-start.12) | collective-permute-done | bytes 524320 | tf_op jit(solution)/shard_map/ppermute | solution.py:259
  138.3 2.8 %collective-permute-start.15 = (bf16[1024,512]{1,0:T(8,128)(2,1)S(1)}, bf16[1024,512]{1,0:T(8,128)(2,1)S(1)}, u32[]{:S(2)}, u32[]{:S(2)}) collective-permute-start(bf16[1024,512]{1,0:T(8,128)(2,1)S(1)} %copy-done.6), channel_id=1, source_target_pairs={{0,2},{1,3},{2,0},{3,1},{4,6},{5,7},{6,4},{7,5},{8,10},{9,11},{10,... | collective-permute-start | bytes 3145736 | tf_op jit(solution)/shard_map/ppermute | solution.py:259
  141.1 2.2 collective-permute-start.16
  143.3 4.6 %collective-permute-done.10.refs_3_ = bf16[512,512]{1,0:T(8,128)(2,1)S(1)} collective-permute-done((bf16[512,512]{1,0:T(8,128)(2,1)}, bf16[512,512]{1,0:T(8,128)(2,1)S(1)}, u32[]{:S(2)}, u32[]{:S(2)}) %collective-permute-start.10) | collective-permute-done | bytes 524320 | tf_op jit(solution)/shard_map/ppermute | solution.py:259
  149.6 2.2 collective-permute-start.7
  154.3 8.9 %shard_map.139.refs_7_ = bf16[512,512]{1,0:T(8,128)(2,1)} custom-call(s32[1]{0:T(128)} %bitcast.base_ref, bf16[8,1280,512]{2,1,0:T(8,128)(2,1)} %get-tuple-element.24.rows_ref, s32[94,128]{1,0:T(8,128)} %get-tuple-element.58.slots_ref, bf16[512,512]{1,0:T(8,128)(2,1)} %copy-done, f32[512,1]{1,0:T(8,128)} %copy.32.mb_ref, bf16[512,512]{1,0:T(8,128)(2,1)} %copy-done.1, ...), custom_call_target="tpu_custom_call" | custom-call | tf_op jit(solution)/shard_map/pallas_call | solution.py:185
  163.9 11.2 %collective-permute-done.7.refs_0_ = bf16[512,512]{1,0:T(8,128)(2,1)} collective-permute-done((bf16[512,512]{1,0:T(8,128)(2,1)}, bf16[512,512]{1,0:T(8,128)(2,1)}, u32[]{:S(2)}, u32[]{:S(2)}) %collective-permute-start.7) | collective-permute-done | bytes 524320 | tf_op jit(solution)/shard_map/ppermute | solution.py:259
  175.1 35.1 %collective-permute-done.15.refs_10_ = bf16[1024,512]{1,0:T(8,128)(2,1)S(1)} collective-permute-done((bf16[1024,512]{1,0:T(8,128)(2,1)S(1)}, bf16[1024,512]{1,0:T(8,128)(2,1)S(1)}, u32[]{:S(2)}, u32[]{:S(2)}) %collective-permute-start.15) | collective-permute-done | bytes 1048608 | tf_op jit(solution)/shard_map/ppermute | solution.py:259
  211.2 10.4 %shard_map.140 = (bf16[512,512]{1,0:T(8,128)(2,1)}, f32[4,1024]{1,0:T(4,128)}, f32[4,1024]{1,0:T(4,128)}) custom-call(bf16[512,512]{1,0:T(8,128)(2,1)} %collective-permute-done.7.refs_0_, bf16[512,512]{1,0:T(8,128)(2,1)} %collective-permute-done.8.refs_1_, bf16[512,512]{1,0:T(8,128)(2,1)} %copy-done.13, bf16[512,512]{1,0:T(8,128)(2,1)} %copy-done.12, ...), custom_call_target="tpu_custom_call" | custom-call | flops 2147483648 | bytes 4194304 | tf_op jit(solution)/shard_map/pallas_call | solution.py:238
  222.6 22.3 %collective-permute-start.18 = (f32[2,1024]{1,0:T(2,128)S(1)}, f32[2,1024]{1,0:T(2,128)S(1)}, u32[]{:S(2)}, u32[]{:S(2)}) collective-permute-start(f32[2,1024]{1,0:T(2,128)S(1)} %bitcast.103), channel_id=1, source_target_pairs={{0,2},{1,3},{2,0},{3,1},{4,6},{5,7},{6,4},{7,5},{8,10},{9,11},{10,... | collective-permute-start | bytes 24584 | tf_op jit(solution)/shard_map/ppermute | solution.py:259
  246.5 3.8 %collective-permute-done.19 = f32[2,1024]{1,0:T(2,128)S(1)} collective-permute-done((f32[2,1024]{1,0:T(2,128)S(1)}, f32[2,1024]{1,0:T(2,128)S(1)}, u32[]{:S(2)}, u32[]{:S(2)}) %collective-permute-start.19) | collective-permute-done | bytes 8224 | tf_op jit(solution)/shard_map/ppermute | solution.py:259
  250.4 8.5 %all-gather = f32[32,2,1024]{2,1,0:T(2,128)S(1)} all-gather(f32[4,2,1024]{2,1,0:T(2,128)S(1)} %pad_maximum_fusion), channel_id=2, replica_groups=mesh['neg'=8,'qry'=4] {'neg'}, dimensions={0}, use_global_device_ids=true | all-gather | bytes 294912 | tf_op jit(solution)/shard_map/all_gather | solution.py:316
  (100 shorter events, 17.5 us)
Async XLA Ops:
  4.3 9.9 %collective-permute-start.5 = (s32[94,128]{1,0:T(8,128)S(1)}, s32[94,128]{1,0:T(8,128)S(1)}, u32[]{:S(2)}, u32[]{:S(2)}) collective-permute-start(s32[94,128]{1,0:T(8,128)S(1)} %get-tuple-element.63), channel_id=1, source_target_pairs={{0,8},{4,12},{8,0},{12,4},{16,24},{20,28},{24,16},{28,20},{1,9},{5... | collective-permute-start | bytes 144392 | tf_op jit(solution)/shard_map/ppermute | solution.py:259
  7.3 7.0 %collective-permute-start.4 = (s32[94,128]{1,0:T(8,128)S(1)}, s32[94,128]{1,0:T(8,128)S(1)}, u32[]{:S(2)}, u32[]{:S(2)}) collective-permute-start(s32[94,128]{1,0:T(8,128)S(1)} %get-tuple-element.62), channel_id=1, source_target_pairs={{0,16},{4,20},{8,24},{12,28},{16,0},{20,4},{24,8},{28,12},{1,17},{... | collective-permute-start | bytes 144392 | tf_op jit(solution)/shard_map/ppermute | solution.py:259
  8.8 5.7 %collective-permute-start.3 = (s32[94,128]{1,0:T(8,128)S(1)}, s32[94,128]{1,0:T(8,128)S(1)}, u32[]{:S(2)}, u32[]{:S(2)}) collective-permute-start(s32[94,128]{1,0:T(8,128)S(1)} %get-tuple-element.61), channel_id=1, source_target_pairs={{0,12},{4,8},{8,4},{12,0},{16,28},{20,24},{24,20},{28,16},{1,13},{... | collective-permute-start | bytes 144392 | tf_op jit(solution)/shard_map/ppermute | solution.py:259
  8.8 5.7 %collective-permute-start.2 = (s32[94,128]{1,0:T(8,128)S(1)}, s32[94,128]{1,0:T(8,128)S(1)}, u32[]{:S(2)}, u32[]{:S(2)}) collective-permute-start(s32[94,128]{1,0:T(8,128)S(1)} %get-tuple-element.60), channel_id=1, source_target_pairs={{0,20},{4,16},{8,28},{12,24},{16,4},{20,0},{24,12},{28,8},{1,21},{... | collective-permute-start | bytes 144392 | tf_op jit(solution)/shard_map/ppermute | solution.py:259
  9.1 5.4 %collective-permute-start.1 = (s32[94,128]{1,0:T(8,128)S(1)}, s32[94,128]{1,0:T(8,128)S(1)}, u32[]{:S(2)}, u32[]{:S(2)}) collective-permute-start(s32[94,128]{1,0:T(8,128)S(1)} %get-tuple-element.59), channel_id=1, source_target_pairs={{0,24},{4,28},{8,16},{12,20},{16,8},{20,12},{24,0},{28,4},{1,25},{... | collective-permute-start | bytes 144392 | tf_op jit(solution)/shard_map/ppermute | solution.py:259
  14.3 54.6 %copy-start.15 = (s32[94,128]{1,0:T(8,128)}, s32[94,128]{1,0:T(8,128)S(1)}, u32[]{:S(2)}) copy-start(s32[94,128]{1,0:T(8,128)S(1)} %collective-permute-done.5.slots_ref) | copy-start | bytes 144388
  14.3 1.2 collective-permute-start.6
  14.3 54.5 %copy-start.16 = (s32[94,128]{1,0:T(8,128)}, s32[94,128]{1,0:T(8,128)S(1)}, u32[]{:S(2)}) copy-start(s32[94,128]{1,0:T(8,128)S(1)} %collective-permute-done.4.slots_ref) | copy-start | bytes 144388
  14.3 4.5 %collective-permute-start = (s32[94,128]{1,0:T(8,128)S(1)}, s32[94,128]{1,0:T(8,128)S(1)}, u32[]{:S(2)}, u32[]{:S(2)}) collective-permute-start(s32[94,128]{1,0:T(8,128)S(1)} %get-tuple-element.65), channel_id=1, source_target_pairs={{0,28},{4,24},{8,20},{12,16},{16,12},{20,8},{24,4},{28,0},{1,29},{... | collective-permute-start | bytes 144392 | tf_op jit(solution)/shard_map/ppermute | solution.py:259
  14.5 54.4 %copy-start.17 = (s32[94,128]{1,0:T(8,128)}, s32[94,128]{1,0:T(8,128)S(1)}, u32[]{:S(2)}) copy-start(s32[94,128]{1,0:T(8,128)S(1)} %collective-permute-done.3.slots_ref) | copy-start | bytes 144388
  14.5 54.4 %copy-start.18 = (s32[94,128]{1,0:T(8,128)}, s32[94,128]{1,0:T(8,128)S(1)}, u32[]{:S(2)}) copy-start(s32[94,128]{1,0:T(8,128)S(1)} %collective-permute-done.2.slots_ref) | copy-start | bytes 144388
  14.5 54.3 %copy-start.19 = (s32[94,128]{1,0:T(8,128)}, s32[94,128]{1,0:T(8,128)S(1)}, u32[]{:S(2)}) copy-start(s32[94,128]{1,0:T(8,128)S(1)} %collective-permute-done.1.slots_ref) | copy-start | bytes 144388
  15.5 53.4 %copy-start.20 = (s32[94,128]{1,0:T(8,128)}, s32[94,128]{1,0:T(8,128)S(1)}, u32[]{:S(2)}) copy-start(s32[94,128]{1,0:T(8,128)S(1)} %collective-permute-done.6.slots_ref) | copy-start | bytes 144388
  18.8 41.2 %copy-start.21 = (s32[94,128]{1,0:T(8,128)}, s32[94,128]{1,0:T(8,128)S(1)}, u32[]{:S(2)}) copy-start(s32[94,128]{1,0:T(8,128)S(1)} %collective-permute-done.slots_ref) | copy-start | bytes 144388
  104.9 22.3 %copy-start.6 = (bf16[1024,512]{1,0:T(8,128)(2,1)S(1)}, bf16[1024,512]{1,0:T(8,128)(2,1)}, u32[]{:S(2)}) copy-start(bf16[1024,512]{1,0:T(8,128)(2,1)} %refs_8_.1) | copy-start | bytes 3145732
  104.9 48.6 %copy-start.22 = (f32[512]{0:T(512)S(1)}, f32[512]{0:T(512)}, u32[]{:S(2)}) copy-start(f32[512]{0:T(512)} %param.22) | copy-start | bytes 6148
  123.1 4.2 %collective-permute-start.13 = (bf16[512,512]{1,0:T(8,128)(2,1)}, bf16[512,512]{1,0:T(8,128)(2,1)S(1)}, u32[]{:S(2)}, u32[]{:S(2)}) collective-permute-start(bf16[512,512]{1,0:T(8,128)(2,1)} %shard_map.138), channel_id=1, source_target_pairs={{0,4},{4,0},{8,12},{12,8},{16,20},{20,16},{24,28},{28,24},{1,5},{5... | collective-permute-start | bytes 1572872 | tf_op jit(solution)/shard_map/ppermute | solution.py:259
  123.5 14.8 %collective-permute-start.12 = (bf16[512,512]{1,0:T(8,128)(2,1)S(1)}, bf16[512,512]{1,0:T(8,128)(2,1)S(1)}, u32[]{:S(2)}, u32[]{:S(2)}) collective-permute-start(bf16[512,512]{1,0:T(8,128)(2,1)S(1)} %copy-done.14), channel_id=1, source_target_pairs={{0,8},{4,12},{8,0},{12,4},{16,24},{20,28},{24,16},{28,20},{1,9},{5... | collective-permute-start | bytes 1572872 | tf_op jit(solution)/shard_map/ppermute | solution.py:259
  124.3 16.8 %collective-permute-start.11 = (bf16[512,512]{1,0:T(8,128)(2,1)}, bf16[512,512]{1,0:T(8,128)(2,1)S(1)}, u32[]{:S(2)}, u32[]{:S(2)}) collective-permute-start(bf16[512,512]{1,0:T(8,128)(2,1)} %shard_map.136), channel_id=1, source_target_pairs={{0,16},{4,20},{8,24},{12,28},{16,0},{20,4},{24,8},{28,12},{1,17},{... | collective-permute-start | bytes 1572872 | tf_op jit(solution)/shard_map/ppermute | solution.py:259
  124.9 22.9 %collective-permute-start.10 = (bf16[512,512]{1,0:T(8,128)(2,1)}, bf16[512,512]{1,0:T(8,128)(2,1)S(1)}, u32[]{:S(2)}, u32[]{:S(2)}) collective-permute-start(bf16[512,512]{1,0:T(8,128)(2,1)} %shard_map.135), channel_id=1, source_target_pairs={{0,12},{4,8},{8,4},{12,0},{16,28},{20,24},{24,20},{28,16},{1,13},{... | collective-permute-start | bytes 1572872 | tf_op jit(solution)/shard_map/ppermute | solution.py:259
  125.6 23.2 %collective-permute-start.9 = (bf16[512,512]{1,0:T(8,128)(2,1)}, bf16[512,512]{1,0:T(8,128)(2,1)S(1)}, u32[]{:S(2)}, u32[]{:S(2)}) collective-permute-start(bf16[512,512]{1,0:T(8,128)(2,1)} %shard_map.134), channel_id=1, source_target_pairs={{0,20},{4,16},{8,28},{12,24},{16,4},{20,0},{24,12},{28,8},{1,21},{... | collective-permute-start | bytes 1572872 | tf_op jit(solution)/shard_map/ppermute | solution.py:259
  127.3 16.0 %copy-start.9 = (bf16[512,512]{1,0:T(8,128)(2,1)}, bf16[512,512]{1,0:T(8,128)(2,1)S(1)}, u32[]{:S(2)}) copy-start(bf16[512,512]{1,0:T(8,128)(2,1)S(1)} %collective-permute-done.13.refs_6_) | copy-start | bytes 1572868
  127.3 47.8 %collective-permute-start.14 = (bf16[1024,512]{1,0:T(8,128)(2,1)S(1)}, bf16[1024,512]{1,0:T(8,128)(2,1)S(1)}, u32[]{:S(2)}, u32[]{:S(2)}) collective-permute-start(bf16[1024,512]{1,0:T(8,128)(2,1)S(1)} %copy-done.6), channel_id=1, source_target_pairs={{0,1},{1,0},{2,3},{3,2},{4,5},{5,4},{6,7},{7,6},{8,9},{9,8},{10,11... | collective-permute-start | bytes 3145736 | tf_op jit(solution)/shard_map/ppermute | solution.py:259
  138.3 9.5 %copy-start.10 = (bf16[512,512]{1,0:T(8,128)(2,1)}, bf16[512,512]{1,0:T(8,128)(2,1)S(1)}, u32[]{:S(2)}) copy-start(bf16[512,512]{1,0:T(8,128)(2,1)S(1)} %collective-permute-done.12.refs_5_) | copy-start | bytes 1572868
  138.3 71.9 %collective-permute-start.15 = (bf16[1024,512]{1,0:T(8,128)(2,1)S(1)}, bf16[1024,512]{1,0:T(8,128)(2,1)S(1)}, u32[]{:S(2)}, u32[]{:S(2)}) collective-permute-start(bf16[1024,512]{1,0:T(8,128)(2,1)S(1)} %copy-done.6), channel_id=1, source_target_pairs={{0,2},{1,3},{2,0},{3,1},{4,6},{5,7},{6,4},{7,5},{8,10},{9,11},{10,... | collective-permute-start | bytes 3145736 | tf_op jit(solution)/shard_map/ppermute | solution.py:259
  141.1 69.1 %collective-permute-start.16 = (bf16[1024,512]{1,0:T(8,128)(2,1)S(1)}, bf16[1024,512]{1,0:T(8,128)(2,1)}, u32[]{:S(2)}, u32[]{:S(2)}) collective-permute-start(bf16[1024,512]{1,0:T(8,128)(2,1)S(1)} %copy-done.6), channel_id=1, source_target_pairs={{0,3},{1,2},{2,1},{3,0},{4,7},{5,6},{6,5},{7,4},{8,11},{9,10},{10,... | collective-permute-start | bytes 3145736 | tf_op jit(solution)/shard_map/ppermute | solution.py:259
  147.8 16.0 %collective-permute-start.8 = (bf16[512,512]{1,0:T(8,128)(2,1)}, bf16[512,512]{1,0:T(8,128)(2,1)}, u32[]{:S(2)}, u32[]{:S(2)}) collective-permute-start(bf16[512,512]{1,0:T(8,128)(2,1)} %shard_map.133), channel_id=1, source_target_pairs={{0,24},{4,28},{8,16},{12,20},{16,8},{20,12},{24,0},{28,4},{1,25},{... | collective-permute-start | bytes 1572872 | tf_op jit(solution)/shard_map/ppermute | solution.py:259
  149.6 25.5 %collective-permute-start.7 = (bf16[512,512]{1,0:T(8,128)(2,1)}, bf16[512,512]{1,0:T(8,128)(2,1)}, u32[]{:S(2)}, u32[]{:S(2)}) collective-permute-start(bf16[512,512]{1,0:T(8,128)(2,1)} %shard_map.132), channel_id=1, source_target_pairs={{0,28},{4,24},{8,20},{12,16},{16,12},{20,8},{24,4},{28,0},{1,29},{... | collective-permute-start | bytes 1572872 | tf_op jit(solution)/shard_map/ppermute | solution.py:259
  175.1 35.1 %copy-start.7 = (bf16[1024,512]{1,0:T(8,128)(2,1)}, bf16[1024,512]{1,0:T(8,128)(2,1)S(1)}, u32[]{:S(2)}) copy-start(bf16[1024,512]{1,0:T(8,128)(2,1)S(1)} %collective-permute-done.14.refs_9_) | copy-start | bytes 3145732
  222.6 23.9 %collective-permute-start.18 = (f32[2,1024]{1,0:T(2,128)S(1)}, f32[2,1024]{1,0:T(2,128)S(1)}, u32[]{:S(2)}, u32[]{:S(2)}) collective-permute-start(f32[2,1024]{1,0:T(2,128)S(1)} %bitcast.103), channel_id=1, source_target_pairs={{0,2},{1,3},{2,0},{3,1},{4,6},{5,7},{6,4},{7,5},{8,10},{9,11},{10,... | collective-permute-start | bytes 24584 | tf_op jit(solution)/shard_map/ppermute | solution.py:259
  244.9 5.4 %collective-permute-start.19 = (f32[2,1024]{1,0:T(2,128)S(1)}, f32[2,1024]{1,0:T(2,128)S(1)}, u32[]{:S(2)}, u32[]{:S(2)}) collective-permute-start(f32[2,1024]{1,0:T(2,128)S(1)} %bitcast.104), channel_id=1, source_target_pairs={{0,3},{1,2},{2,1},{3,0},{4,7},{5,6},{6,5},{7,4},{8,11},{9,10},{10,... | collective-permute-start | bytes 24584 | tf_op jit(solution)/shard_map/ppermute | solution.py:259
  245.5 4.9 %collective-permute-start.17 = (f32[2,1024]{1,0:T(2,128)S(1)}, f32[2,1024]{1,0:T(2,128)S(1)}, u32[]{:S(2)}, u32[]{:S(2)}) collective-permute-start(f32[2,1024]{1,0:T(2,128)S(1)} %bitcast.105), channel_id=1, source_target_pairs={{0,1},{1,0},{2,3},{3,2},{4,5},{5,4},{6,7},{7,6},{8,9},{9,8},{10,11... | collective-permute-start | bytes 24584 | tf_op jit(solution)/shard_map/ppermute | solution.py:259
  (11 other events, 25.5 us)
where the time goes:
time: 261 us; the launch traced here: 260 us
  Pallas kernels  118 us (45%)
  waiting for transfers between devices  69.2 us (27%)
  starting transfers between devices  45.4 us (17%)
  local copies, waits for them, and re-layouts  12.9 us (5%)
  blocking collectives  8.52 us (3%)
  other arithmetic  4.82 us (2%)
    pallas_call x8, Pallas kernels, partial_hidden(): pl.pallas_call(partial_kernel, grid=(1,), out_shape=jax.ShapeDtypeStruct(...  72 us
    ppermute x20, waiting for transfers between devices, swap(): return lax.ppermute(value, axis, [(i, i ^ offset) for i in range(size)])  69.2 us
    ppermute x20, starting transfers between devices, swap(): return lax.ppermute(value, axis, [(i, i ^ offset) for i in range(size)])  45.4 us
    pallas_call x1, Pallas kernels, gather_rows(): pl.pallas_call(gather_kernel, grid=(blocks,), out_shape=[jax.ShapeDtypeSt...  35.5 us
    pallas_call x1, Pallas kernels, embed_and_score(): pl.pallas_call(functools.partial(score_kernel, len(parts), blocks), out_s...  10.4 us
    all_gather x1, blocking collectives, per_device(): pairs = lax.all_gather(pairs, 'neg').reshape(n_neg * n_qry, 2, -1)  8.52 us
    unnamed x64, local copies, waits for them, and re-layouts  7.48 us
  transfers between devices with their start and end apart: 20, of which 9 were waited for; matrix products, arithmetic and copies ran while one was open for 2% of the time, Pallas kernels for 3%

commit v1 on v0

--- a/solution.py
+++ b/solution.py
@@ -58,11 +58,12 @@
 
     @pl.loop(0, cap // unroll)
     def _(i):
+        first = block * cap + i * unroll
+        start = pl.multiple_of(i * (unroll * pieces), unroll * pieces)
+        places = [pl.multiple_of(index_ref[first + u], pieces) for u in range(unroll)]
         for u in range(unroll):
-            place = i * unroll + u
-            row = pl.multiple_of(index_ref[block, place], pieces)
-            picked_ref[pl.ds(pl.multiple_of(place * pieces, pieces), pieces), :] = wide_ref[
-                pl.ds(row, pieces), :
+            picked_ref[pl.ds(start + u * pieces, pieces), :] = wide_ref[
+                pl.ds(places[u], pieces), :
             ]
 
     @pl.loop(0, cap // ROWS)
@@ -74,8 +75,8 @@
             ].astype(jnp.bfloat16)
 
 
-def gather_rows(index, table, weights):
-    blocks, cap = index.shape
+def gather_rows(index, cap, table, weights):
+    blocks = index.shape[0] // cap
     rows, width = table.shape
     pieces = width // LANES
     return pl.pallas_call(
@@ -295,9 +296,9 @@
         query_blocks.append(swap(queries, "qry", d))
 
     base = (own_neg * cap).astype(jnp.int32).reshape(1)
-    wanted = jnp.stack([asked[d][(half + 1) * groups :].reshape(cap) for d in far])
+    wanted = jnp.concatenate([asked[d][(half + 1) * groups :].reshape(cap) for d in far])
     rows, wm, ws, wn = gather_rows(
-        wanted, items_table, (message_weight, self_weight, neighbour_weight)
+        wanted, cap, items_table, (message_weight, self_weight, neighbour_weight)
     )
     parts = []
     for j, d in enumerate(far):

time: 261 us -> 244 us (0.935)
  Pallas kernels: 118 us -> 101 us
    pallas_call x1, Pallas kernels: 35.5 us -> 18.8 us  [gather_rows(): pl.pallas_call(gather_kernel, grid=(blocks,), out_shape=[jax.ShapeDtypeSt...]
    unnamed x64 -> x57, local copies, waits for them, and re-layouts: 7.48 us -> 7.44 us
  transfers between devices with their start and end apart: 20 -> 20, of which waited for: 9 -> 9; matrix products, arithmetic and copies ran while one was open for 2% -> 2% of each run, Pallas kernels for 3% -> 4%
where the time goes in v1:
time: 244 us; the launch traced here: 243 us
  Pallas kernels  101 us (41%)
  waiting for transfers between devices  68.2 us (28%)
  starting transfers between devices  45.8 us (19%)
  local copies, waits for them, and re-layouts  12.8 us (5%)
  blocking collectives  9.52 us (4%)
  other arithmetic  4.82 us (2%)
    pallas_call x8, Pallas kernels, partial_hidden(): pl.pallas_call(partial_kernel, grid=(1,), out_shape=jax.ShapeDtypeStruct(...  72 us
    ppermute x20, waiting for transfers between devices, swap(): return lax.ppermute(value, axis, [(i, i ^ offset) for i in range(size)])  68.2 us
    ppermute x20, starting transfers between devices, swap(): return lax.ppermute(value, axis, [(i, i ^ offset) for i in range(size)])  45.8 us
    pallas_call x1, Pallas kernels, gather_rows(): pl.pallas_call(gather_kernel, grid=(blocks,), out_shape=[jax.ShapeDtypeSt...  18.8 us
    pallas_call x1, Pallas kernels, embed_and_score(): pl.pallas_call(functools.partial(score_kernel, len(parts), blocks), out_s...  10.4 us
    all_gather x1, blocking collectives, per_device(): pairs = lax.all_gather(pairs, 'neg').reshape(n_neg * n_qry, 2, -1)  9.52 us
    unnamed x57, local copies, waits for them, and re-layouts  7.44 us
  transfers between devices with their start and end apart: 20, of which 9 were waited for; matrix products, arithmetic and copies ran while one was open for 2% of the time, Pallas kernels for 4%

profile of v1, /device:TPU:0, one launch (start us, length us, event | category | flops | bytes accessed | tf_op | source)
XLA Modules:
  0.0 243.3 jit_solution(17129152451836319569)
XLA Ops:
  1.6 1.4 dynamic-slice_reduce_fusion
  3.7 3.4 %collective-permute-start = (s32[94,128]{1,0:T(8,128)S(1)}, s32[94,128]{1,0:T(8,128)S(1)}, u32[]{:S(2)}, u32[]{:S(2)}) collective-permute-start(s32[94,128]{1,0:T(8,128)S(1)} %get-tuple-element.64), channel_id=1, source_target_pairs={{0,28},{4,24},{8,20},{12,16},{16,12},{20,8},{24,4},{28,0},{1,29},{... | collective-permute-start | bytes 144392 | tf_op jit(solution)/shard_map/ppermute | solution.py:260
  7.1 1.3 pad_add_fusion.8
  8.9 1.4 collective-permute-start.2
  10.4 1.2 collective-permute-start.3
  12.1 1.5 copy.32.mb_ref
  15.7 2.1 collective-permute-done.5.slots_ref
  20.9 18.8 %shard_map.131 = (bf16[8,1280,512]{2,1,0:T(8,128)(2,1)}, bf16[512,512]{1,0:T(8,128)(2,1)S(1)}, bf16[512,512]{1,0:T(8,128)(2,1)S(1)}, bf16[512,512]{1,0:T(8,128)(2,1)S(1)}) custom-call(s32[10240]{0:T(1024)S(1)} %broadcast_multiply_fusion.index_ref, bf16[8192,512]{1,0:T(8,128)(2,1)} %table_ref.1, bf16[512,512]{1,0:T(8,128)(2,1)S(1)} %copy-done.3, ...), custom_call_target="tpu_custom_call" | custom-call | tf_op jit(solution)/shard_map/pallas_call | solution.py:82
  42.2 8.9 %shard_map.132 = bf16[512,512]{1,0:T(8,128)(2,1)} custom-call(s32[1]{0:T(128)} %bitcast.base_ref, bf16[8,1280,512]{2,1,0:T(8,128)(2,1)} %get-tuple-element.24.rows_ref, s32[94,128]{1,0:T(8,128)} %copy-done.15, bf16[512,512]{1,0:T(8,128)(2,1)} %copy-done, f32[512,1]{1,0:T(8,128)} %copy.32.mb_ref, bf16[512,512]{1,0:T(8,128)(2,1)} %copy-done.1, ...), custom_call_target="tpu_custom_call" | custom-call | tf_op jit(solution)/shard_map/pallas_call | solution.py:186
  51.1 9.0 %shard_map.133 = bf16[512,512]{1,0:T(8,128)(2,1)} custom-call(s32[1]{0:T(128)} %bitcast.base_ref, bf16[8,1280,512]{2,1,0:T(8,128)(2,1)} %get-tuple-element.24.rows_ref, s32[94,128]{1,0:T(8,128)} %copy-done.16, bf16[512,512]{1,0:T(8,128)(2,1)} %copy-done, f32[512,1]{1,0:T(8,128)} %copy.32.mb_ref, bf16[512,512]{1,0:T(8,128)(2,1)} %copy-done.1, ...), custom_call_target="tpu_custom_call" | custom-call | tf_op jit(solution)/shard_map/pallas_call | solution.py:186
  60.1 9.0 %shard_map.134 = bf16[512,512]{1,0:T(8,128)(2,1)} custom-call(s32[1]{0:T(128)} %bitcast.base_ref, bf16[8,1280,512]{2,1,0:T(8,128)(2,1)} %get-tuple-element.24.rows_ref, s32[94,128]{1,0:T(8,128)} %copy-done.17, bf16[512,512]{1,0:T(8,128)(2,1)} %copy-done, f32[512,1]{1,0:T(8,128)} %copy.32.mb_ref, bf16[512,512]{1,0:T(8,128)(2,1)} %copy-done.1, ...), custom_call_target="tpu_custom_call" | custom-call | tf_op jit(solution)/shard_map/pallas_call | solution.py:186
  69.2 9.1 %shard_map.135 = bf16[512,512]{1,0:T(8,128)(2,1)} custom-call(s32[1]{0:T(128)} %bitcast.base_ref, bf16[8,1280,512]{2,1,0:T(8,128)(2,1)} %get-tuple-element.24.rows_ref, s32[94,128]{1,0:T(8,128)} %copy-done.18, bf16[512,512]{1,0:T(8,128)(2,1)} %copy-done, f32[512,1]{1,0:T(8,128)} %copy.32.mb_ref, bf16[512,512]{1,0:T(8,128)(2,1)} %copy-done.1, ...), custom_call_target="tpu_custom_call" | custom-call | tf_op jit(solution)/shard_map/pallas_call | solution.py:186
  78.2 8.9 %shard_map.136 = bf16[512,512]{1,0:T(8,128)(2,1)} custom-call(s32[1]{0:T(128)} %bitcast.base_ref, bf16[8,1280,512]{2,1,0:T(8,128)(2,1)} %get-tuple-element.24.rows_ref, s32[94,128]{1,0:T(8,128)} %copy-done.19, bf16[512,512]{1,0:T(8,128)(2,1)} %copy-done, f32[512,1]{1,0:T(8,128)} %copy.32.mb_ref, bf16[512,512]{1,0:T(8,128)(2,1)} %copy-done.1, ...), custom_call_target="tpu_custom_call" | custom-call | tf_op jit(solution)/shard_map/pallas_call | solution.py:186
  87.2 9.1 %shard_map.137 = bf16[512,512]{1,0:T(8,128)(2,1)} custom-call(s32[1]{0:T(128)} %bitcast.base_ref, bf16[8,1280,512]{2,1,0:T(8,128)(2,1)} %get-tuple-element.24.rows_ref, s32[94,128]{1,0:T(8,128)} %copy-done.20, bf16[512,512]{1,0:T(8,128)(2,1)} %copy-done, f32[512,1]{1,0:T(8,128)} %copy.32.mb_ref, bf16[512,512]{1,0:T(8,128)(2,1)} %copy-done.1, ...), custom_call_target="tpu_custom_call" | custom-call | tf_op jit(solution)/shard_map/pallas_call | solution.py:186
  96.3 9.1 %shard_map.138 = bf16[512,512]{1,0:T(8,128)(2,1)} custom-call(s32[1]{0:T(128)} %bitcast.base_ref, bf16[8,1280,512]{2,1,0:T(8,128)(2,1)} %get-tuple-element.24.rows_ref, s32[94,128]{1,0:T(8,128)} %copy-done.21, bf16[512,512]{1,0:T(8,128)(2,1)} %copy-done, f32[512,1]{1,0:T(8,128)} %copy.32.mb_ref, bf16[512,512]{1,0:T(8,128)(2,1)} %copy-done.1, ...), custom_call_target="tpu_custom_call" | custom-call | tf_op jit(solution)/shard_map/pallas_call | solution.py:186
  106.3 1.4 collective-permute-start.11
  109.2 1.6 collective-permute-start.14
  110.8 9.4 %collective-permute-done.12.refs_5_ = bf16[512,512]{1,0:T(8,128)(2,1)S(1)} collective-permute-done((bf16[512,512]{1,0:T(8,128)(2,1)S(1)}, bf16[512,512]{1,0:T(8,128)(2,1)S(1)}, u32[]{:S(2)}, u32[]{:S(2)}) %collective-permute-start.12) | collective-permute-done | bytes 524320 | tf_op jit(solution)/shard_map/ppermute | solution.py:260
  120.2 3.1 %collective-permute-start.15 = (bf16[1024,512]{1,0:T(8,128)(2,1)S(1)}, bf16[1024,512]{1,0:T(8,128)(2,1)S(1)}, u32[]{:S(2)}, u32[]{:S(2)}) collective-permute-start(bf16[1024,512]{1,0:T(8,128)(2,1)S(1)} %copy-done.6), channel_id=1, source_target_pairs={{0,2},{1,3},{2,0},{3,1},{4,6},{5,7},{6,4},{7,5},{8,10},{9,11},{10,... | collective-permute-start | bytes 3145736 | tf_op jit(solution)/shard_map/ppermute | solution.py:260
  123.3 1.6 collective-permute-start.16
  125.0 5.4 %collective-permute-done.10.refs_3_ = bf16[512,512]{1,0:T(8,128)(2,1)S(1)} collective-permute-done((bf16[512,512]{1,0:T(8,128)(2,1)}, bf16[512,512]{1,0:T(8,128)(2,1)S(1)}, u32[]{:S(2)}, u32[]{:S(2)}) %collective-permute-start.10) | collective-permute-done | bytes 524320 | tf_op jit(solution)/shard_map/ppermute | solution.py:260
  130.4 1.8 collective-permute-start.8
  133.0 1.8 collective-permute-start.7
  137.3 8.9 %shard_map.139.refs_7_ = bf16[512,512]{1,0:T(8,128)(2,1)} custom-call(s32[1]{0:T(128)} %bitcast.base_ref, bf16[8,1280,512]{2,1,0:T(8,128)(2,1)} %get-tuple-element.24.rows_ref, s32[94,128]{1,0:T(8,128)} %get-tuple-element.57.slots_ref, bf16[512,512]{1,0:T(8,128)(2,1)} %copy-done, f32[512,1]{1,0:T(8,128)} %copy.32.mb_ref, bf16[512,512]{1,0:T(8,128)(2,1)} %copy-done.1, ...), custom_call_target="tpu_custom_call" | custom-call | tf_op jit(solution)/shard_map/pallas_call | solution.py:186
  146.4 10.6 %collective-permute-done.7.refs_0_ = bf16[512,512]{1,0:T(8,128)(2,1)} collective-permute-done((bf16[512,512]{1,0:T(8,128)(2,1)}, bf16[512,512]{1,0:T(8,128)(2,1)}, u32[]{:S(2)}, u32[]{:S(2)}) %collective-permute-start.7) | collective-permute-done | bytes 524320 | tf_op jit(solution)/shard_map/ppermute | solution.py:260
  157.0 35.3 %collective-permute-done.15.refs_10_ = bf16[1024,512]{1,0:T(8,128)(2,1)S(1)} collective-permute-done((bf16[1024,512]{1,0:T(8,128)(2,1)S(1)}, bf16[1024,512]{1,0:T(8,128)(2,1)S(1)}, u32[]{:S(2)}, u32[]{:S(2)}) %collective-permute-start.15) | collective-permute-done | bytes 1048608 | tf_op jit(solution)/shard_map/ppermute | solution.py:260
  193.3 10.4 %shard_map.140 = (bf16[512,512]{1,0:T(8,128)(2,1)}, f32[4,1024]{1,0:T(4,128)}, f32[4,1024]{1,0:T(4,128)}) custom-call(bf16[512,512]{1,0:T(8,128)(2,1)} %collective-permute-done.7.refs_0_, bf16[512,512]{1,0:T(8,128)(2,1)} %collective-permute-done.8.refs_1_, bf16[512,512]{1,0:T(8,128)(2,1)} %copy-done.13, bf16[512,512]{1,0:T(8,128)(2,1)} %copy-done.12, ...), custom_call_target="tpu_custom_call" | custom-call | flops 2147483648 | bytes 4194304 | tf_op jit(solution)/shard_map/pallas_call | solution.py:239
  204.7 20.7 %collective-permute-start.17 = (f32[2,1024]{1,0:T(2,128)S(1)}, f32[2,1024]{1,0:T(2,128)S(1)}, u32[]{:S(2)}, u32[]{:S(2)}) collective-permute-start(f32[2,1024]{1,0:T(2,128)S(1)} %bitcast.82), channel_id=1, source_target_pairs={{0,1},{1,0},{2,3},{3,2},{4,5},{5,4},{6,7},{7,6},{8,9},{9,8},{10,11... | collective-permute-start | bytes 24584 | tf_op jit(solution)/shard_map/ppermute | solution.py:260
  225.4 2.1 collective-permute-start.18
  227.4 1.5 collective-permute-start.19
  230.0 2.9 %collective-permute-done.19 = f32[2,1024]{1,0:T(2,128)S(1)} collective-permute-done((f32[2,1024]{1,0:T(2,128)S(1)}, f32[2,1024]{1,0:T(2,128)S(1)}, u32[]{:S(2)}, u32[]{:S(2)}) %collective-permute-start.19) | collective-permute-done | bytes 8224 | tf_op jit(solution)/shard_map/ppermute | solution.py:260
  232.9 9.5 %all-gather = f32[32,2,1024]{2,1,0:T(2,128)S(1)} all-gather(f32[4,2,1024]{2,1,0:T(2,128)S(1)} %pad_maximum_fusion), channel_id=2, replica_groups=mesh['neg'=8,'qry'=4] {'neg'}, dimensions={0}, use_global_device_ids=true | all-gather | bytes 294912 | tf_op jit(solution)/shard_map/all_gather | solution.py:317
  (94 shorter events, 20.2 us)
Async XLA Ops:
  3.7 9.9 %collective-permute-start = (s32[94,128]{1,0:T(8,128)S(1)}, s32[94,128]{1,0:T(8,128)S(1)}, u32[]{:S(2)}, u32[]{:S(2)}) collective-permute-start(s32[94,128]{1,0:T(8,128)S(1)} %get-tuple-element.64), channel_id=1, source_target_pairs={{0,28},{4,24},{8,20},{12,16},{16,12},{20,8},{24,4},{28,0},{1,29},{... | collective-permute-start | bytes 144392 | tf_op jit(solution)/shard_map/ppermute | solution.py:260
  8.4 5.9 %collective-permute-start.1 = (s32[94,128]{1,0:T(8,128)S(1)}, s32[94,128]{1,0:T(8,128)S(1)}, u32[]{:S(2)}, u32[]{:S(2)}) collective-permute-start(s32[94,128]{1,0:T(8,128)S(1)} %get-tuple-element.58), channel_id=1, source_target_pairs={{0,24},{4,28},{8,16},{12,20},{16,8},{20,12},{24,0},{28,4},{1,25},{... | collective-permute-start | bytes 144392 | tf_op jit(solution)/shard_map/ppermute | solution.py:260
  8.9 5.4 %collective-permute-start.2 = (s32[94,128]{1,0:T(8,128)S(1)}, s32[94,128]{1,0:T(8,128)S(1)}, u32[]{:S(2)}, u32[]{:S(2)}) collective-permute-start(s32[94,128]{1,0:T(8,128)S(1)} %get-tuple-element.59), channel_id=1, source_target_pairs={{0,20},{4,16},{8,28},{12,24},{16,4},{20,0},{24,12},{28,8},{1,21},{... | collective-permute-start | bytes 144392 | tf_op jit(solution)/shard_map/ppermute | solution.py:260
  10.4 4.1 %collective-permute-start.3 = (s32[94,128]{1,0:T(8,128)S(1)}, s32[94,128]{1,0:T(8,128)S(1)}, u32[]{:S(2)}, u32[]{:S(2)}) collective-permute-start(s32[94,128]{1,0:T(8,128)S(1)} %get-tuple-element.60), channel_id=1, source_target_pairs={{0,12},{4,8},{8,4},{12,0},{16,28},{20,24},{24,20},{28,16},{1,13},{... | collective-permute-start | bytes 144392 | tf_op jit(solution)/shard_map/ppermute | solution.py:260
  11.6 4.1 %collective-permute-start.4 = (s32[94,128]{1,0:T(8,128)S(1)}, s32[94,128]{1,0:T(8,128)S(1)}, u32[]{:S(2)}, u32[]{:S(2)}) collective-permute-start(s32[94,128]{1,0:T(8,128)S(1)} %get-tuple-element.61), channel_id=1, source_target_pairs={{0,16},{4,20},{8,24},{12,28},{16,0},{20,4},{24,8},{28,12},{1,17},{... | collective-permute-start | bytes 144392 | tf_op jit(solution)/shard_map/ppermute | solution.py:260
  13.6 28.5 %copy-start.15 = (s32[94,128]{1,0:T(8,128)}, s32[94,128]{1,0:T(8,128)S(1)}, u32[]{:S(2)}) copy-start(s32[94,128]{1,0:T(8,128)S(1)} %collective-permute-done.slots_ref) | copy-start | bytes 144388
  13.6 4.1 %collective-permute-start.5 = (s32[94,128]{1,0:T(8,128)S(1)}, s32[94,128]{1,0:T(8,128)S(1)}, u32[]{:S(2)}, u32[]{:S(2)}) collective-permute-start(s32[94,128]{1,0:T(8,128)S(1)} %get-tuple-element.62), channel_id=1, source_target_pairs={{0,8},{4,12},{8,0},{12,4},{16,24},{20,28},{24,16},{28,20},{1,9},{5... | collective-permute-start | bytes 144392 | tf_op jit(solution)/shard_map/ppermute | solution.py:260
  14.3 36.8 %copy-start.16 = (s32[94,128]{1,0:T(8,128)}, s32[94,128]{1,0:T(8,128)S(1)}, u32[]{:S(2)}) copy-start(s32[94,128]{1,0:T(8,128)S(1)} %collective-permute-done.1.slots_ref) | copy-start | bytes 144388
  14.3 3.5 %collective-permute-start.6 = (s32[94,128]{1,0:T(8,128)S(1)}, s32[94,128]{1,0:T(8,128)S(1)}, u32[]{:S(2)}, u32[]{:S(2)}) collective-permute-start(s32[94,128]{1,0:T(8,128)S(1)} %get-tuple-element.63), channel_id=1, source_target_pairs={{0,4},{4,0},{8,12},{12,8},{16,20},{20,16},{24,28},{28,24},{1,5},{5... | collective-permute-start | bytes 144392 | tf_op jit(solution)/shard_map/ppermute | solution.py:260
  14.4 36.7 %copy-start.17 = (s32[94,128]{1,0:T(8,128)}, s32[94,128]{1,0:T(8,128)S(1)}, u32[]{:S(2)}) copy-start(s32[94,128]{1,0:T(8,128)S(1)} %collective-permute-done.2.slots_ref) | copy-start | bytes 144388
  14.4 36.6 %copy-start.18 = (s32[94,128]{1,0:T(8,128)}, s32[94,128]{1,0:T(8,128)S(1)}, u32[]{:S(2)}) copy-start(s32[94,128]{1,0:T(8,128)S(1)} %collective-permute-done.3.slots_ref) | copy-start | bytes 144388
  15.7 35.4 %copy-start.19 = (s32[94,128]{1,0:T(8,128)}, s32[94,128]{1,0:T(8,128)S(1)}, u32[]{:S(2)}) copy-start(s32[94,128]{1,0:T(8,128)S(1)} %collective-permute-done.4.slots_ref) | copy-start | bytes 144388
  17.7 33.3 %copy-start.20 = (s32[94,128]{1,0:T(8,128)}, s32[94,128]{1,0:T(8,128)S(1)}, u32[]{:S(2)}) copy-start(s32[94,128]{1,0:T(8,128)S(1)} %collective-permute-done.5.slots_ref) | copy-start | bytes 144388
  17.8 33.3 %copy-start.21 = (s32[94,128]{1,0:T(8,128)}, s32[94,128]{1,0:T(8,128)S(1)}, u32[]{:S(2)}) copy-start(s32[94,128]{1,0:T(8,128)S(1)} %collective-permute-done.6.slots_ref) | copy-start | bytes 144388
  87.2 22.0 %copy-start.6 = (bf16[1024,512]{1,0:T(8,128)(2,1)S(1)}, bf16[1024,512]{1,0:T(8,128)(2,1)}, u32[]{:S(2)}) copy-start(bf16[1024,512]{1,0:T(8,128)(2,1)} %refs_8_.1) | copy-start | bytes 3145732
  87.2 49.2 %copy-start.22 = (f32[512]{0:T(512)S(1)}, f32[512]{0:T(512)}, u32[]{:S(2)}) copy-start(f32[512]{0:T(512)} %param.22) | copy-start | bytes 6148
  105.3 3.8 %collective-permute-start.13 = (bf16[512,512]{1,0:T(8,128)(2,1)}, bf16[512,512]{1,0:T(8,128)(2,1)S(1)}, u32[]{:S(2)}, u32[]{:S(2)}) collective-permute-start(bf16[512,512]{1,0:T(8,128)(2,1)} %shard_map.138), channel_id=1, source_target_pairs={{0,4},{4,0},{8,12},{12,8},{16,20},{20,16},{24,28},{28,24},{1,5},{5... | collective-permute-start | bytes 1572872 | tf_op jit(solution)/shard_map/ppermute | solution.py:260
  105.3 14.9 %collective-permute-start.12 = (bf16[512,512]{1,0:T(8,128)(2,1)S(1)}, bf16[512,512]{1,0:T(8,128)(2,1)S(1)}, u32[]{:S(2)}, u32[]{:S(2)}) collective-permute-start(bf16[512,512]{1,0:T(8,128)(2,1)S(1)} %copy-done.14), channel_id=1, source_target_pairs={{0,8},{4,12},{8,0},{12,4},{16,24},{20,28},{24,16},{28,20},{1,9},{5... | collective-permute-start | bytes 1572872 | tf_op jit(solution)/shard_map/ppermute | solution.py:260
  106.3 17.0 %collective-permute-start.11 = (bf16[512,512]{1,0:T(8,128)(2,1)}, bf16[512,512]{1,0:T(8,128)(2,1)S(1)}, u32[]{:S(2)}, u32[]{:S(2)}) collective-permute-start(bf16[512,512]{1,0:T(8,128)(2,1)} %shard_map.136), channel_id=1, source_target_pairs={{0,16},{4,20},{8,24},{12,28},{16,0},{20,4},{24,8},{28,12},{1,17},{... | collective-permute-start | bytes 1572872 | tf_op jit(solution)/shard_map/ppermute | solution.py:260
  107.8 22.6 %collective-permute-start.10 = (bf16[512,512]{1,0:T(8,128)(2,1)}, bf16[512,512]{1,0:T(8,128)(2,1)S(1)}, u32[]{:S(2)}, u32[]{:S(2)}) collective-permute-start(bf16[512,512]{1,0:T(8,128)(2,1)} %shard_map.135), channel_id=1, source_target_pairs={{0,12},{4,8},{8,4},{12,0},{16,28},{20,24},{24,20},{28,16},{1,13},{... | collective-permute-start | bytes 1572872 | tf_op jit(solution)/shard_map/ppermute | solution.py:260
  108.9 23.3 %collective-permute-start.9 = (bf16[512,512]{1,0:T(8,128)(2,1)}, bf16[512,512]{1,0:T(8,128)(2,1)S(1)}, u32[]{:S(2)}, u32[]{:S(2)}) collective-permute-start(bf16[512,512]{1,0:T(8,128)(2,1)} %shard_map.134), channel_id=1, source_target_pairs={{0,20},{4,16},{8,28},{12,24},{16,4},{20,0},{24,12},{28,8},{1,21},{... | collective-permute-start | bytes 1572872 | tf_op jit(solution)/shard_map/ppermute | solution.py:260
  109.2 15.8 %copy-start.9 = (bf16[512,512]{1,0:T(8,128)(2,1)}, bf16[512,512]{1,0:T(8,128)(2,1)S(1)}, u32[]{:S(2)}) copy-start(bf16[512,512]{1,0:T(8,128)(2,1)S(1)} %collective-permute-done.13.refs_6_) | copy-start | bytes 1572868
  109.2 47.8 %collective-permute-start.14 = (bf16[1024,512]{1,0:T(8,128)(2,1)S(1)}, bf16[1024,512]{1,0:T(8,128)(2,1)S(1)}, u32[]{:S(2)}, u32[]{:S(2)}) collective-permute-start(bf16[1024,512]{1,0:T(8,128)(2,1)S(1)} %copy-done.6), channel_id=1, source_target_pairs={{0,1},{1,0},{2,3},{3,2},{4,5},{5,4},{6,7},{7,6},{8,9},{9,8},{10,11... | collective-permute-start | bytes 3145736 | tf_op jit(solution)/shard_map/ppermute | solution.py:260
  120.2 10.2 %copy-start.10 = (bf16[512,512]{1,0:T(8,128)(2,1)}, bf16[512,512]{1,0:T(8,128)(2,1)S(1)}, u32[]{:S(2)}) copy-start(bf16[512,512]{1,0:T(8,128)(2,1)S(1)} %collective-permute-done.12.refs_5_) | copy-start | bytes 1572868
  120.2 72.1 %collective-permute-start.15 = (bf16[1024,512]{1,0:T(8,128)(2,1)S(1)}, bf16[1024,512]{1,0:T(8,128)(2,1)S(1)}, u32[]{:S(2)}, u32[]{:S(2)}) collective-permute-start(bf16[1024,512]{1,0:T(8,128)(2,1)S(1)} %copy-done.6), channel_id=1, source_target_pairs={{0,2},{1,3},{2,0},{3,1},{4,6},{5,7},{6,4},{7,5},{8,10},{9,11},{10,... | collective-permute-start | bytes 3145736 | tf_op jit(solution)/shard_map/ppermute | solution.py:260
  123.3 68.9 %collective-permute-start.16 = (bf16[1024,512]{1,0:T(8,128)(2,1)S(1)}, bf16[1024,512]{1,0:T(8,128)(2,1)}, u32[]{:S(2)}, u32[]{:S(2)}) collective-permute-start(bf16[1024,512]{1,0:T(8,128)(2,1)S(1)} %copy-done.6), channel_id=1, source_target_pairs={{0,3},{1,2},{2,1},{3,0},{4,7},{5,6},{6,5},{7,4},{8,11},{9,10},{10,... | collective-permute-start | bytes 3145736 | tf_op jit(solution)/shard_map/ppermute | solution.py:260
  130.4 16.0 %collective-permute-start.8 = (bf16[512,512]{1,0:T(8,128)(2,1)}, bf16[512,512]{1,0:T(8,128)(2,1)}, u32[]{:S(2)}, u32[]{:S(2)}) collective-permute-start(bf16[512,512]{1,0:T(8,128)(2,1)} %shard_map.133), channel_id=1, source_target_pairs={{0,24},{4,28},{8,16},{12,20},{16,8},{20,12},{24,0},{28,4},{1,25},{... | collective-permute-start | bytes 1572872 | tf_op jit(solution)/shard_map/ppermute | solution.py:260
  133.0 24.0 %collective-permute-start.7 = (bf16[512,512]{1,0:T(8,128)(2,1)}, bf16[512,512]{1,0:T(8,128)(2,1)}, u32[]{:S(2)}, u32[]{:S(2)}) collective-permute-start(bf16[512,512]{1,0:T(8,128)(2,1)} %shard_map.132), channel_id=1, source_target_pairs={{0,28},{4,24},{8,20},{12,16},{16,12},{20,8},{24,4},{28,0},{1,29},{... | collective-permute-start | bytes 1572872 | tf_op jit(solution)/shard_map/ppermute | solution.py:260
  157.0 35.3 %copy-start.7 = (bf16[1024,512]{1,0:T(8,128)(2,1)}, bf16[1024,512]{1,0:T(8,128)(2,1)S(1)}, u32[]{:S(2)}) copy-start(bf16[1024,512]{1,0:T(8,128)(2,1)S(1)} %collective-permute-done.14.refs_9_) | copy-start | bytes 3145732
  204.7 24.2 %collective-permute-start.17 = (f32[2,1024]{1,0:T(2,128)S(1)}, f32[2,1024]{1,0:T(2,128)S(1)}, u32[]{:S(2)}, u32[]{:S(2)}) collective-permute-start(f32[2,1024]{1,0:T(2,128)S(1)} %bitcast.82), channel_id=1, source_target_pairs={{0,1},{1,0},{2,3},{3,2},{4,5},{5,4},{6,7},{7,6},{8,9},{9,8},{10,11... | collective-permute-start | bytes 24584 | tf_op jit(solution)/shard_map/ppermute | solution.py:260
  225.4 4.6 %collective-permute-start.18 = (f32[2,1024]{1,0:T(2,128)S(1)}, f32[2,1024]{1,0:T(2,128)S(1)}, u32[]{:S(2)}, u32[]{:S(2)}) collective-permute-start(f32[2,1024]{1,0:T(2,128)S(1)} %bitcast.83), channel_id=1, source_target_pairs={{0,2},{1,3},{2,0},{3,1},{4,6},{5,7},{6,4},{7,5},{8,10},{9,11},{10,... | collective-permute-start | bytes 24584 | tf_op jit(solution)/shard_map/ppermute | solution.py:260
  227.4 5.4 %collective-permute-start.19 = (f32[2,1024]{1,0:T(2,128)S(1)}, f32[2,1024]{1,0:T(2,128)S(1)}, u32[]{:S(2)}, u32[]{:S(2)}) collective-permute-start(f32[2,1024]{1,0:T(2,128)S(1)} %bitcast.84), channel_id=1, source_target_pairs={{0,3},{1,2},{2,1},{3,0},{4,7},{5,6},{6,5},{7,4},{8,11},{9,10},{10,... | collective-permute-start | bytes 24584 | tf_op jit(solution)/shard_map/ppermute | solution.py:260
  (11 other events, 27.1 us)
